TPU v7x, 32 devices: a whole 2x2x4 slice. The times are simulated.
32 devices in a mesh: leaf: 8 (over z, y), blk: 4 (over x, core).
Axes of the slice: x: 2, y: 2, z: 4, core: 2. Of those that a mesh axis runs over, the one named last changes fastest.
Arguments:
- src_pos: int32 [4, 2097152], P('blk', 'leaf'), may hold values from 0 to 8388607, as said below
- strengths: float32 [2, 4, 2097152], P(None, 'blk', 'leaf'), may hold values from -0.001953125 to 0.001953125
- tgt_pos: int32 [8388608], P(('leaf', 'blk')), may hold values from 0 to 201326591, as said below
Outputs:
- field: float32 [2, 8388608], P(None, ('leaf', 'blk'))
Inputs may be any that keep to these rules, and one draw needn't show every extreme that they name: `src_pos`: row q holds 16384 runs of 128 cells; run b lies in the 128 cells from (q * 16384 + b) * 128 on. `tgt_pos`: the ticks held by index k of leaf, at every index of blk, come in 2048 runs of 128; run j lies in the 12288 ticks from (j * 8 + r) * 12288 on, where r is k with its 3 binary digits in reverse order.
All inputs are finite; a program needn't handle non-finite values.
Results may differ from a plain program's by a relative error of at most 0.0003.
Values sent between devices are 32-bit elements; how exact they have to be, the bound alone decides.
No kernel may reach another device: no remote copies, remote signals or barrier semaphores. Data moves between devices by JAX's collectives and lax.ppermute only.
A program may use at most 128 MiB of HBM per device.

v0:
```python
import functools

import jax
import jax.numpy as jnp
import numpy as np
from jax import lax
from jax.experimental import pallas as pl
from jax.experimental.pallas import tpu as pltpu
from jax.sharding import PartitionSpec as P


R = 16
PER_BOX = 128
TGT_BOX = 128
BOX_CELLS = 128
TOP_TICKS = 201326592
LANES = 128
ROWS = 2 * R
HALF = R // 2
CHUNKS = 2
PHASE_SHARES = ((6, 0), (2, 0), (4, 1), (4, 1))
PHASE_PLAN = {"bit_0": (0,), "bit_1": (1,), "last": (2, 3)}
LEAF_STEPS = 4

SIN_COEFS = (4.44288292, -7.30824569, 3.60635422, -0.84611165, 0.10982452)
COS_COEFS = (1.4142135, -6.97885095, 5.73946038, -1.88355791, 0.31068803)


def node_offsets(box_cells):
    node_index = np.arange(R)
    unit_nodes = (1.0 - np.cos(np.pi * (node_index + 0.5) / R)) / 2.0
    return np.floor(box_cells * unit_nodes).astype(np.int64)


def lagrange_values(node_pos, points):
    basis_rows = []
    for row_node in range(node_pos.shape[0]):
        column = np.ones(points.shape[0])
        for other_node in range(node_pos.shape[0]):
            if other_node != row_node:
                column = (
                    column
                    * (points - node_pos[other_node])
                    / (node_pos[row_node] - node_pos[other_node])
                )
        basis_rows.append(column)
    return np.stack(basis_rows)


def turn_exp(ticks, cells):
    product = (ticks * cells) % 2**32
    return np.exp(2j * np.pi * (product / 2.0**32))


def as_real(matrix):
    return np.block([[matrix.real, -matrix.imag], [matrix.imag, matrix.real]])


def level_blocks(tree_level):
    child_cells = BOX_CELLS * 2**tree_level
    box_ticks = TOP_TICKS // 2**tree_level
    assert box_ticks // 2 * child_cells % 2**32 == 0
    child_nodes = node_offsets(child_cells)
    parent_nodes = node_offsets(2 * child_cells)
    inner_cells = np.concatenate([child_nodes, child_nodes + child_cells])
    blend = lagrange_values(
        parent_nodes / (2.0 * child_cells), inner_cells / (2.0 * child_cells)
    ).reshape(R, 2, R)
    blend = blend.astype(np.float32).astype(np.float64)
    center = box_ticks // 4
    return [
        [
            blend[:, child]
            * turn_exp((2 * half - 1) * (box_ticks // 4), child_nodes)[None, :]
            * turn_exp(center, child * child_cells)
            for child in range(2)
        ]
        for half in range(2)
    ]


def stage_matrix(first_level, order):
    count = len(order)
    size = 2**count
    levels = [level_blocks(first_level + step) for step in range(count)]
    place = [order.index(step) for step in range(count)]
    full = np.zeros((size, ROWS, size, ROWS))
    for out_block in range(size):
        for in_block in range(size):
            matrix = np.eye(R)
            for step in range(count):
                bits = (out_block >> place[step] & 1, in_block >> place[step] & 1)
                matrix = levels[step][bits[0]][bits[1]] @ matrix
            full[out_block, :, in_block, :] = as_real(matrix)
    return full


def product_basis():
    table = np.zeros((R, R))
    for high in range(4):
        for low in range(4):
            for degree in (4 * high + low, abs(4 * high - low)):
                table[4 * high + low, degree] += 0.5
    return table


def leaf_matrix():
    leaf_nodes = node_offsets(BOX_CELLS)
    node_angles = np.pi * (np.arange(R) + 0.5) / R
    at_exact = lagrange_values(2.0 * leaf_nodes / BOX_CELLS - 1.0, np.cos(node_angles))
    cheb_at = np.stack([np.cos(degree * node_angles) for degree in range(R)])
    norm_weights = np.where(np.arange(R) == 0, 1.0, 2.0) / R
    coefficients = norm_weights[:, None] * (cheb_at @ at_exact.T)
    coefficients = coefficients.astype(np.float32).astype(np.float64)
    return as_real(coefficients.T @ np.linalg.inv(product_basis()))


def field_rows():
    table = np.zeros((4, HALF, 2, R))
    for node in range(HALF):
        mirror = R - 1 - node
        table[0, node, 0, [node, mirror]] = 1.0
        table[1, node, 1, [node, mirror]] = [1.0, -1.0]
        table[2, node, 1, [node, mirror]] = 1.0
        table[3, node, 0, [node, mirror]] = [-1.0, 1.0]
    return table.reshape(ROWS, ROWS)


def split_table(matrix):
    high = matrix.astype(np.float32).astype(jnp.bfloat16)
    low = (matrix - high.astype(np.float64)).astype(np.float32).astype(jnp.bfloat16)
    return np.concatenate([high, high, low], axis=-1)


def split_value(value):
    high = value.astype(jnp.bfloat16)
    low = (value - high.astype(jnp.float32)).astype(jnp.bfloat16)
    return jnp.concatenate([high, low, high], axis=0)


def times_table(table, value):
    return jnp.dot(table, split_value(value), preferred_element_type=jnp.float32)


def polynomial(coefs, value):
    total = jnp.full_like(value, coefs[-1])
    for coef in coefs[-2::-1]:
        total = total * value + coef
    return total


def unit_circle(turns):
    rest = turns - jnp.round(turns)
    square = rest * rest
    sine = rest * polynomial(SIN_COEFS, square)
    cosine = polynomial(COS_COEFS, square)
    return 1.0 - sine * sine, sine * cosine


def reverse_bits(value, count):
    return sum((value >> bit & 1) << (count - 1 - bit) for bit in range(count))


def swap_bits(blocks, block_bit, lane_bit):
    step = 1 << lane_bit
    shape = blocks[0].shape
    upper = (lax.broadcasted_iota(jnp.int32, shape, 1) >> lane_bit & 1) == 1
    swapped = list(blocks)
    for number in range(len(blocks)):
        if not number >> block_bit & 1:
            other = number | 1 << block_bit
            low, high = blocks[number], blocks[other]
            swapped[number] = jnp.where(upper, pltpu.roll(high, step, 1), low)
            swapped[other] = jnp.where(upper, high, pltpu.roll(low, LANES - step, 1))
    return swapped


def run_stage(blocks, row_bits, table):
    count = len(blocks)
    side_bits = [bit for bit in range(count.bit_length() - 1) if bit not in row_bits]

    def number(row, side):
        return sum((row >> k & 1) << bit for k, bit in enumerate(row_bits)) + sum(
            (side >> k & 1) << bit for k, bit in enumerate(side_bits)
        )

    sides = range(2 ** len(side_bits))
    rows = range(2 ** len(row_bits))
    value = jnp.concatenate(
        [
            jnp.concatenate([blocks[number(row, side)] for row in rows], axis=0)
            for side in sides
        ],
        axis=1,
    )
    product = times_table(table, value)
    result = list(blocks)
    for side in sides:
        for row in rows:
            result[number(row, side)] = product[
                row * ROWS : (row + 1) * ROWS, side * LANES : (side + 1) * LANES
            ]
    return result


def cell_table():
    turned = turn_exp(TOP_TICKS // 2, np.arange(BOX_CELLS))
    return jnp.asarray(np.repeat([turned.real, turned.imag], 8, axis=0), jnp.float32)


def pick_lanes(table, lanes):
    numbers = lax.GatherDimensionNumbers(
        offset_dims=(),
        collapsed_slice_dims=(1,),
        start_index_map=(1,),
        operand_batching_dims=(0,),
        start_indices_batching_dims=(0,),
    )
    return lax.gather(
        table, lanes[..., None], numbers, (1, 1), mode=lax.GatherScatterMode.PROMISE_IN_BOUNDS
    )


def leaf_kernel(pos_ref, strength_ref, table_ref, *refs):
    count = (len(refs) - 2) // 2
    out_ref, semaphores = refs[count], refs[-1]
    copies = [
        pltpu.make_async_copy(source, target, semaphores.at[number])
        for number, (source, target) in enumerate(zip(refs[:count], refs[count + 1 : -1]))
    ]

    @pl.when(pl.program_id(0) == 0)
    def start_copies():
        for copy in copies:
            copy.start()

    tile_count = pos_ref.shape[0] // LANES
    first = pl.program_id(0) * tile_count

    def one_tile(tile, carry):
        parts = [[], [], []]
        for group in range(16):
            start = tile * LANES + 8 * reverse_bits(group, 4)
            rows = pl.ds(pl.multiple_of(start, 8), 8)
            parts[0].append(pos_ref[rows, :] & (BOX_CELLS - 1))
            parts[1].append(strength_ref[0, rows, :])
            parts[2].append(strength_ref[1, rows, :])
        cells, real, imag = (jnp.concatenate(part, axis=0).T for part in parts)
        sums = [None] * ROWS
        for group in range(16):
            rows = slice(8 * group, 8 * group + 8)
            turn = [pick_lanes(table_ref[8 * row : 8 * row + 8, :], cells[rows]) for row in range(2)]
            turned = complex_product(turn, (real[rows], imag[rows]))
            v = cells[rows].astype(jnp.float32) * (2.0 / BOX_CELLS) - 1.0
            t2 = 2.0 * (v * v) - 1.0
            t3 = v * (2.0 * t2 - 1.0)
            t4 = 2.0 * (t2 * t2) - 1.0
            t8 = 2.0 * (t4 * t4) - 1.0
            t12 = t4 * (2.0 * t8 - 1.0)
            for side, value in enumerate(turned):
                for high, outer in enumerate((None, t4, t8, t12)):
                    base = value if outer is None else value * outer
                    for low, inner in enumerate((None, v, t2, t3)):
                        term = base if inner is None else base * inner
                        row = side * R + 4 * high + low
                        sums[row] = term if sums[row] is None else sums[row] + term
        for row in range(ROWS):
            out_ref[first + tile, pl.ds(row, 1), :] = jnp.sum(sums[row], axis=0, keepdims=True)
        return carry

    lax.fori_loop(0, tile_count, one_tile, 0, unroll=4)

    @pl.when(pl.program_id(0) == pl.num_programs(0) - 1)
    def wait_copies():
        for copy in copies:
            copy.wait()


def tree_kernel(moment_ref, t1_ref, t2_ref, t3_ref, t4_ref, *out_refs):
    tile_count = moment_ref.shape[0]
    blocks = [moment_ref[tile] for tile in range(tile_count)]
    for block_bit, lane_bit in ((0, 2), (1, 1), (2, 0)):
        blocks = swap_bits(blocks, block_bit, lane_bit)
    blocks = run_stage(blocks, (0, 1, 2), t1_ref[...])
    for block_bit, lane_bit in ((2, 6), (1, 5), (0, 4)):
        blocks = swap_bits(blocks, block_bit, lane_bit)
    blocks = run_stage(blocks, (0, 1, 2), t2_ref[...])
    for block_bit, lane_bit in ((2, 3), (1, 2), (0, 1)):
        blocks = swap_bits(blocks, block_bit, lane_bit)
    blocks = run_stage(blocks, (0, 1, 2), t3_ref[...])
    blocks = swap_bits(blocks, 2, 0)
    blocks = run_stage(blocks, (2, 3), t4_ref[...])
    for block_bit, lane_bit in ((3, 3), (2, 4), (0, 5), (1, 6)):
        blocks = swap_bits(blocks, block_bit, lane_bit)
    for number in range(tile_count):
        place = sum((number >> bit & 1) << to for bit, to in ((1, 3), (0, 2), (2, 1), (3, 0)))
        part, column = divmod(place, tile_count // len(out_refs))
        out_refs[part][:, column * LANES : (column + 1) * LANES] = blocks[number]


def source_tables():
    first = stage_matrix(0, [2, 1, 0])
    first = np.einsum("abcd,de->abce", first, leaf_matrix())
    second = stage_matrix(3, [2, 1, 0])
    third = stage_matrix(6, [2, 1, 0])
    fourth = stage_matrix(9, [0, 1])
    return [
        jnp.asarray(split_table(table.reshape(len(table) * ROWS, -1)))
        for table in (first, second, third, fourth)
    ]


def join_kernel(own_ref, partner_ref, table_ref, out_ref, *, bit_no):
    side = lax.axis_index("leaf") >> bit_no & 1
    value = jnp.concatenate([own_ref[...], partner_ref[...]], axis=0)
    out_ref[...] = times_table(table_ref[side], value)


def join_table(tree_level, last):
    blocks = level_blocks(tree_level)
    sides = []
    for side in range(2):
        table = np.concatenate(
            [as_real(blocks[side][side]), as_real(blocks[side][1 - side])], axis=1
        )
        sides.append(split_table(field_rows() @ table if last else table))
    return jnp.asarray(np.stack(sides))


def box_rows(first):
    return pl.ds(first, 8, stride=16)


def complex_product(left, right):
    return left[0] * right[0] - left[1] * right[1], left[0] * right[1] + left[1] * right[0]


def square_of(value):
    double = 2.0 * value[1]
    return 1.0 - double * value[1], double * value[0]


def target_phases(offsets, group_cells, pair_count):
    rates = (group_cells - 1 - 2 * node_offsets(group_cells)[:HALF]) / 2.0**33
    found = [unit_circle(offsets * float(rate)) for rate in rates]
    middle = unit_circle(offsets * float((group_cells - 1) / 2.0**33))
    step = unit_circle(offsets * float(group_cells / 2.0**32))
    twice = square_of(step)
    found += [step, middle]
    for _ in range(1, pair_count):
        found.append(complex_product(found[-1], twice))
    return found


def phase_kernel(tgt_ref, after_ref, out_ref, *, first_tile, leaf_count, group_cells, pair_count):
    box_ticks = TOP_TICKS // (group_cells // BOX_CELLS)
    leaf_no = lax.axis_index("leaf")
    leaf_bits = leaf_count.bit_length() - 1
    low_box = sum((leaf_no >> bit & 1) << (leaf_bits - 1 - bit) for bit in range(leaf_bits))
    base = low_box * box_ticks + box_ticks // 2

    def one_tile(tile, carry):
        ticks = [tgt_ref[box_rows((tile + first_tile) * LANES + group), :] for group in range(16)]
        ticks = jnp.concatenate(ticks, axis=0)
        lane = lax.broadcasted_iota(jnp.int32, ticks.shape, 0)
        box = (lane & 7) * 16 + (lane >> 3) + (tile + first_tile) * LANES
        center = box * (leaf_count * box_ticks) + base
        offsets = (ticks - center).astype(jnp.float32).T
        for number, (cosine, sine) in enumerate(target_phases(offsets, group_cells, pair_count)):
            out_ref[tile, 2 * number] = cosine
            out_ref[tile, 2 * number + 1] = sine
        return carry

    lax.fori_loop(0, out_ref.shape[0], one_tile, 0, unroll=2)


def block_sums(phase_ref, roots, tile, first):
    totals = [None, None]
    for node in range(HALF):
        for wave in range(2):
            phase = phase_ref[tile, 2 * node + wave]
            for side in range(2):
                row = first + (2 * side + wave) * HALF + node
                term = phase * roots[pl.ds(row, 1), :]
                totals[side] = term if totals[side] is None else totals[side] + term
    return totals


def pair_field(phase_ref, root_refs, roots, sums, tile, column, pair, add_ref=None):
    low = lax.axis_index("blk") & 1
    for number, root_ref in enumerate(root_refs):
        rows = pl.ds((low ^ number) * ROWS, ROWS)
        roots[rows, :] = root_ref[:, pl.ds(pl.multiple_of(column, LANES), LANES)]
    for side, total in enumerate(block_sums(phase_ref, roots, tile, ROWS)):
        sums[side] = total
    totals = block_sums(phase_ref, roots, tile, 0)
    step = phase_ref[tile, 2 * HALF], phase_ref[tile, 2 * HALF + 1]
    real, imag = complex_product(step, (sums[0], sums[1]))
    plane = 2 * HALF + 2 + 2 * pair
    start = phase_ref[tile, plane], phase_ref[tile, plane + 1]
    values = complex_product(start, (real + totals[0], imag + totals[1]))
    for side, value in enumerate(values):
        sums[side] = value if add_ref is None else value + add_ref[side]


def near_kernel(phase_ref, *refs, first_column):
    root_refs, (out_ref, roots) = refs[:2], refs[2:]
    pair = lax.axis_index("blk") >> 1

    def one_tile(tile, carry):
        column = (tile + first_column) * LANES
        pair_field(phase_ref, root_refs, roots, out_ref.at[tile], tile, column, pair)
        return carry

    lax.fori_loop(0, out_ref.shape[0], one_tile, 0)


def share_places(tile_counts):
    firsts = [sum(tile_counts[:part]) for part in range(len(tile_counts))]
    starts = {}
    for (_, chunk), first in zip(PHASE_SHARES, firsts):
        starts.setdefault(chunk, first)
    return firsts, [first - starts[chunk] for (_, chunk), first in zip(PHASE_SHARES, firsts)]


def far_kernel(*refs, masks):
    count = len(PHASE_SHARES)
    phase_refs, near_refs, root_refs = refs[:count], refs[count : 2 * count], refs[2 * count : -5]
    out_ref, roots, sums, rows_ref, semaphores = refs[-5:]
    firsts, places = share_places([near_ref.shape[0] for near_ref in near_refs])

    def out_copy(number):
        rows = pl.ds(pl.multiple_of(number * 2 * LANES, 2 * LANES), 2 * LANES)
        return pltpu.make_async_copy(
            rows_ref.at[number], out_ref.at[rows, :], semaphores.at[number]
        )

    def make(number, tile, part):
        chunk = PHASE_SHARES[part][1]
        column = (places[part] + tile) * LANES
        found = root_refs[chunk * len(masks) : (chunk + 1) * len(masks)]
        add_ref = near_refs[part].at[tile]
        for first in range(0, len(masks), 2):
            pair = (lax.axis_index("blk") ^ masks[first]) >> 1
            out = sums.at[number & 1]
            pair_roots = found[first : first + 2]
            pair_field(phase_refs[part], pair_roots, roots, out, tile, column, pair, add_ref)
            add_ref = out

    def put(number):
        for side in range(2):
            values = sums[number & 1, side].T
            for group in range(16):
                rows = pl.ds(2 * group + side, 8, stride=32)
                rows_ref[number, rows, :] = values[8 * group : 8 * group + 8]

    make(0, 0, 0)
    for part in range(count):

        def one_tile(tile, carry, part=part):
            number = firsts[part] + tile
            put(number - 1)
            make(number, tile, part)
            out_copy(number - 1).start()
            return carry

        lax.fori_loop(1 if part == 0 else 0, near_refs[part].shape[0], one_tile, 0)
    last = rows_ref.shape[0] - 1
    put(last)
    out_copy(last).start()
    for number in range(last + 1):
        out_copy(number).wait()


small_vmem = pltpu.CompilerParams(vmem_limit_bytes=6 * 2**20)


def in_vmem(value):
    return pltpu.with_memory_space_constraint(value, pltpu.VMEM)


def in_hbm(value):
    return pltpu.with_memory_space_constraint(value, pltpu.HBM)


def whole_vmem(count):
    return [pl.BlockSpec(memory_space=pltpu.VMEM)] * count


def partner_2(block, axis, apart):
    count = lax.axis_size(axis)
    route = []
    for low in range(count):
        high = low | 1 << apart
        if high != low and high < count:
            route += [(low, high), (high, low)]
    return lax.ppermute(block, axis, route)


def local(src_pos, strengths, tgt_pos):
    leaf_count = lax.axis_size("leaf")
    leaf_bits = leaf_count.bit_length() - 1
    box_count = src_pos.shape[1] // PER_BOX
    local_depth = box_count.bit_length() - 1
    assert box_count == 16 * LANES
    group_cells = box_count * leaf_count * BOX_CELLS
    box_ticks = TOP_TICKS // (box_count * leaf_count)
    offsets = node_offsets(group_cells)
    assert (offsets + offsets[::-1] == group_cells - 1).all()
    assert box_ticks // 2 * group_cells % 2**32 == 0

    tile_count = box_count // LANES
    part_tiles = [tile_count * share // 16 for share, _ in PHASE_SHARES]
    firsts, places = share_places(part_tiles)

    leaf_rows = box_count // LEAF_STEPS
    tables = source_tables() + [
        join_table(local_depth + bit_no, bit_no == leaf_bits - 1) for bit_no in range(leaf_bits)
    ]
    copied = [*tables, tgt_pos.reshape(box_count, TGT_BOX)]
    moments, *copied = pl.pallas_call(
        leaf_kernel,
        grid=(LEAF_STEPS,),
        out_shape=[pltpu.VMEM((tile_count, ROWS, LANES), jnp.float32)]
        + [pltpu.VMEM(value.shape, value.dtype) for value in copied],
        in_specs=[
            pl.BlockSpec((leaf_rows, PER_BOX), lambda i: (i, 0)),
            pl.BlockSpec((2, leaf_rows, PER_BOX), lambda i: (0, i, 0)),
            pl.BlockSpec((16, BOX_CELLS), lambda i: (0, 0)),
        ]
        + [pl.BlockSpec(memory_space=pl.ANY)] * len(copied),
        out_specs=whole_vmem(1 + len(copied)),
        scratch_shapes=[pltpu.SemaphoreType.DMA((len(copied),))],
        compiler_params=small_vmem,
        name="leaves",
    )(
        in_hbm(src_pos.reshape(box_count, PER_BOX)),
        in_hbm(strengths.reshape(2, box_count, PER_BOX)),
        in_hbm(cell_table()),
        *[in_hbm(value) for value in copied],
    )
    *tables, ticks = copied
    parts = pl.pallas_call(
        tree_kernel,
        out_shape=[pltpu.VMEM((ROWS, box_count // CHUNKS), jnp.float32)] * CHUNKS,
        in_specs=whole_vmem(5),
        out_specs=whole_vmem(CHUNKS),
        compiler_params=small_vmem,
        name="tree",
    )(in_vmem(moments), *[in_vmem(table) for table in tables[:-leaf_bits]])

    blk_count = lax.axis_size("blk")
    blk_bits = blk_count.bit_length() - 1
    plane_count = 2 * HALF + 2 + blk_count

    def make_phases(number, after):
        return pl.pallas_call(
            functools.partial(
                phase_kernel,
                first_tile=firsts[number],
                leaf_count=leaf_count,
                group_cells=group_cells,
                pair_count=blk_count // 2,
            ),
            out_shape=pltpu.VMEM((part_tiles[number], plane_count, TGT_BOX, LANES), jnp.float32),
            in_specs=whole_vmem(1) + [pl.BlockSpec(memory_space=pl.ANY)],
            out_specs=pl.BlockSpec(memory_space=pltpu.VMEM),
            compiler_params=small_vmem,
            name="phases",
        )(in_vmem(ticks), after)

    def join(part, partner, bit_no):
        return pl.pallas_call(
            functools.partial(join_kernel, bit_no=bit_no),
            out_shape=pltpu.VMEM(part.shape, jnp.float32),
            in_specs=whole_vmem(3),
            out_specs=pl.BlockSpec(memory_space=pltpu.VMEM),
            compiler_params=small_vmem,
            name="join",
        )(in_vmem(part), in_vmem(partner), in_vmem(tables[bit_no - leaf_bits]))

    def near_field(number, roots):
        return pl.pallas_call(
            functools.partial(near_kernel, first_column=places[number]),
            out_shape=pltpu.VMEM((part_tiles[number], 2, TGT_BOX, LANES), jnp.float32),
            in_specs=whole_vmem(3),
            out_specs=pl.BlockSpec(memory_space=pltpu.VMEM),
            scratch_shapes=[pltpu.VMEM((2 * ROWS, LANES), jnp.float32)],
            compiler_params=small_vmem,
            name="near",
        )(in_vmem(phases[number]), *[in_vmem(root) for root in roots])

    phases = []
    for bit_no in range(leaf_bits):
        stage = "last" if bit_no == leaf_bits - 1 else f"bit_{bit_no}"
        partners = []
        for part in parts:
            partners.append(partner_2(part, "leaf", bit_no))
        for number in PHASE_PLAN.get(stage, ()):
            phases.append(make_phases(number, parts[0]))
            partners[0], phases[-1] = lax.optimization_barrier((partners[0], phases[-1]))
        joined = []
        for part, partner in zip(parts, partners):
            joined.append(join(part, partner, bit_no))
        parts = joined
    masks = list(range(2, blk_count))
    founds = []
    for part in parts:
        found = {0: part, 1: partner_2(part, "blk", 0)}
        for blk_bit in range(1, blk_bits):
            found[1 << blk_bit] = partner_2(part, "blk", blk_bit)
        founds.append(found)
    near = []
    for number, (_, chunk) in enumerate(PHASE_SHARES):
        near.append(near_field(number, (founds[chunk][0], founds[chunk][1])))
    founds[0][2], *near[:3] = lax.optimization_barrier((founds[0][2], *near[:3]))
    founds[1][2], near[3] = lax.optimization_barrier((founds[1][2], near[3]))
    for found in founds:
        for mask in masks:
            if mask not in found:
                low_bit = mask & -mask
                found[mask] = partner_2(
                    found[mask ^ low_bit], "blk", low_bit.bit_length() - 1
                )
    operands = [*phases, *near, *[found[mask] for found in founds for mask in masks]]
    field = pl.pallas_call(
        functools.partial(far_kernel, masks=masks),
        out_shape=jax.ShapeDtypeStruct((2 * box_count, TGT_BOX), jnp.float32),
        in_specs=whole_vmem(len(operands)),
        out_specs=pl.BlockSpec(memory_space=pl.ANY),
        scratch_shapes=[
            pltpu.VMEM((2 * ROWS, LANES), jnp.float32),
            pltpu.VMEM((2, 2, TGT_BOX, LANES), jnp.float32),
            pltpu.VMEM((tile_count, 2 * LANES, TGT_BOX), jnp.float32),
            pltpu.SemaphoreType.DMA((tile_count,)),
        ],
        compiler_params=small_vmem,
        name="far",
    )(*[in_vmem(value) for value in operands])
    field = field.reshape(box_count, 2, TGT_BOX)
    return jnp.transpose(field, (1, 0, 2)).reshape(2, box_count * TGT_BOX)


def solution(mesh):
    return jax.shard_map(
        local,
        mesh=mesh,
        in_specs=(P("blk", "leaf"), P(None, "blk", "leaf"), P(("leaf", "blk"))),
        out_specs=P(None, ("leaf", "blk")),
        check_vma=False,
    )
```

profile of v0, /device:TPU:0, one launch (start us, length us, event | category | flops | bytes accessed | tf_op | source)
XLA Modules:
  0.0 52.2 jit_solution(3876085795099363693)
XLA Ops:
  0.0 5.8 %leaves.1 = (f32[16,32,128]{2,1,0:T(8,128)S(1)}, bf16[256,768]{1,0:T(8,128)(2,1)S(1)}, bf16[256,768]{1,0:T(8,128)(2,1)S(1)}, bf16[256,768]{1,0:T(8,128)(2,1)S(1)...) custom-call(s32[2048,128]{1,0:T(8,128)} %bitcast.9, ...), custom_call_target="tpu_custom_call" | custom-call | tf_op jit(solution)/shard_map/leaves/pallas_call | solution.py:521
  5.8 2.3 %tree.1 = (f32[32,1024]{1,0:T(8,128)S(1)}, f32[32,1024]{1,0:T(8,128)S(1)}) custom-call(f32[16,32,128]{2,1,0:T(8,128)S(1)} %get-tuple-element.30.moment_ref, bf16[256,768]{1,0:T(8,128)(2,1)S(1)} %get-tuple-element.31.t1_ref, bf16[256,768]{1,0:T(8,128)(2,1)S(1)} %get-tuple-element.32.t2_ref, bf16[256,768]{1,0:T(8,128)(2,1)S(1)} %get-tuple-element.33.t3_ref, ...), custom_call_target="tpu_custom_call" | custom-call | tf_op jit(solution)/shard_map/tree/pallas_call | solution.py:543
  8.1 3.1 %collective-permute-start.5 = (f32[32,1024]{1,0:T(8,128)S(1)}, f32[32,1024]{1,0:T(8,128)S(1)}, u32[]{:S(2)}, u32[]{:S(2)}) collective-permute-start(f32[32,1024]{1,0:T(8,128)S(1)} %get-tuple-element.48.own_ref), channel_id=1, source_target_pairs={{0,4},{4,0},{8,12},{12,8},{16,20},{20,16},{24,28},{28,24},{1,5},{5... | collective-permute-start | bytes 393224 | tf_op jit(solution)/shard_map/ppermute | solution.py:497
  11.1 0.1 collective-permute-start
  11.2 3.7 %phases.4.phase_ref.refs_0_ = f32[6,22,128,128]{3,2,1,0:T(8,128)S(1)} custom-call(s32[2048,128]{1,0:T(8,128)S(1)} %get-tuple-element.36.tgt_ref, f32[32,1024]{1,0:T(8,128)S(1)} %get-tuple-element.35.after_ref.own_ref), custom_call_target="tpu_custom_call" | custom-call | tf_op jit(solution)/shard_map/phases/pallas_call | solution.py:557
  15.0 0.5 collective-permute-done.5.partner_ref
  15.5 0.2 join.9.own_ref
  15.7 2.1 %collective-permute-start.6 = (f32[32,1024]{1,0:T(8,128)S(1)}, f32[32,1024]{1,0:T(8,128)S(1)}, u32[]{:S(2)}, u32[]{:S(2)}) collective-permute-start(f32[32,1024]{1,0:T(8,128)S(1)} %join.9.own_ref), channel_id=1, source_target_pairs={{0,8},{8,0},{4,12},{12,4},{16,24},{24,16},{20,28},{28,20},{1,9},{9... | collective-permute-start | bytes 393224 | tf_op jit(solution)/shard_map/ppermute | solution.py:497
  17.8 0.0 collective-permute-done.partner_ref
  17.8 0.2 join.6.after_ref.own_ref
  18.0 1.5 %collective-permute-start.1 = (f32[32,1024]{1,0:T(8,128)S(1)}, f32[32,1024]{1,0:T(8,128)S(1)}, u32[]{:S(2)}, u32[]{:S(2)}) collective-permute-start(f32[32,1024]{1,0:T(8,128)S(1)} %join.6.after_ref.own_ref), channel_id=1, source_target_pairs={{0,8},{8,0},{4,12},{12,4},{16,24},{24,16},{20,28},{28,20},{1,9},{9... | collective-permute-start | bytes 393224 | tf_op jit(solution)/shard_map/ppermute | solution.py:497
  19.5 1.2 %phases.5.phase_ref.refs_1_ = f32[2,22,128,128]{3,2,1,0:T(8,128)S(1)} custom-call(s32[2048,128]{1,0:T(8,128)S(1)} %get-tuple-element.36.tgt_ref, f32[32,1024]{1,0:T(8,128)S(1)} %join.6.after_ref.own_ref), custom_call_target="tpu_custom_call" | custom-call | tf_op jit(solution)/shard_map/phases/pallas_call | solution.py:557
  20.7 1.3 %collective-permute-done.6.partner_ref = f32[32,1024]{1,0:T(8,128)S(1)} collective-permute-done((f32[32,1024]{1,0:T(8,128)S(1)}, f32[32,1024]{1,0:T(8,128)S(1)}, u32[]{:S(2)}, u32[]{:S(2)}) %collective-permute-start.6) | collective-permute-done | bytes 131104 | tf_op jit(solution)/shard_map/ppermute | solution.py:497
  21.9 0.2 join.10.own_ref
  22.1 3.3 %collective-permute-start.7 = (f32[32,1024]{1,0:T(8,128)S(1)}, f32[32,1024]{1,0:T(8,128)S(1)}, u32[]{:S(2)}, u32[]{:S(2)}) collective-permute-start(f32[32,1024]{1,0:T(8,128)S(1)} %join.10.own_ref), channel_id=1, source_target_pairs={{0,16},{16,0},{4,20},{20,4},{8,24},{24,8},{12,28},{28,12},{1,17},{... | collective-permute-start | bytes 393224 | tf_op jit(solution)/shard_map/ppermute | solution.py:497
  25.4 0.0 collective-permute-done.1.partner_ref
  25.4 0.2 join.7.after_ref.own_ref
  25.6 2.6 %collective-permute-start.2 = (f32[32,1024]{1,0:T(8,128)S(1)}, f32[32,1024]{1,0:T(8,128)S(1)}, u32[]{:S(2)}, u32[]{:S(2)}) collective-permute-start(f32[32,1024]{1,0:T(8,128)S(1)} %join.7.after_ref.own_ref), channel_id=1, source_target_pairs={{0,16},{16,0},{4,20},{20,4},{8,24},{24,8},{12,28},{28,12},{1,17},{... | collective-permute-start | bytes 393224 | tf_op jit(solution)/shard_map/ppermute | solution.py:497
  28.2 2.5 %phases.7.phase_ref.refs_3_ = f32[4,22,128,128]{3,2,1,0:T(8,128)S(1)} custom-call(s32[2048,128]{1,0:T(8,128)S(1)} %get-tuple-element.36.tgt_ref, f32[32,1024]{1,0:T(8,128)S(1)} %join.7.after_ref.own_ref), custom_call_target="tpu_custom_call" | custom-call | tf_op jit(solution)/shard_map/phases/pallas_call | solution.py:557
  30.7 2.5 %phases.6.phase_ref.refs_2_ = f32[4,22,128,128]{3,2,1,0:T(8,128)S(1)} custom-call(s32[2048,128]{1,0:T(8,128)S(1)} %get-tuple-element.36.tgt_ref, f32[32,1024]{1,0:T(8,128)S(1)} %join.7.after_ref.own_ref), custom_call_target="tpu_custom_call" | custom-call | tf_op jit(solution)/shard_map/phases/pallas_call | solution.py:557
  33.2 0.3 collective-permute-done.7.partner_ref
  33.5 0.2 join.11.refs_0_
  33.7 1.4 %collective-permute-start.9 = (f32[32,1024]{1,0:T(8,128)S(1)}, f32[32,1024]{1,0:T(8,128)S(1)}, u32[]{:S(2)}, u32[]{:S(2)}) collective-permute-start(f32[32,1024]{1,0:T(8,128)S(1)} %join.11.refs_0_), channel_id=1, source_target_pairs={{0,2},{2,0},{1,3},{3,1},{4,6},{6,4},{5,7},{7,5},{8,10},{10,8},{9,1... | collective-permute-start | bytes 393224 | tf_op jit(solution)/shard_map/ppermute | solution.py:497
  35.0 0.0 collective-permute-start.8
  35.0 0.0 collective-permute-done.2.partner_ref
  35.0 0.2 join.8.refs_0_
  35.2 0.6 %collective-permute-start.4 = (f32[32,1024]{1,0:T(8,128)S(1)}, f32[32,1024]{1,0:T(8,128)S(1)}, u32[]{:S(2)}, u32[]{:S(2)}) collective-permute-start(f32[32,1024]{1,0:T(8,128)S(1)} %join.8.refs_0_), channel_id=1, source_target_pairs={{0,1},{1,0},{2,3},{3,2},{4,5},{5,4},{6,7},{7,6},{8,9},{9,8},{10,11... | collective-permute-start | bytes 393224 | tf_op jit(solution)/shard_map/ppermute | solution.py:497
  35.8 0.7 %collective-permute-start.3 = (f32[32,1024]{1,0:T(8,128)S(1)}, f32[32,1024]{1,0:T(8,128)S(1)}, u32[]{:S(2)}, u32[]{:S(2)}) collective-permute-start(f32[32,1024]{1,0:T(8,128)S(1)} %join.8.refs_0_), channel_id=1, source_target_pairs={{0,2},{2,0},{1,3},{3,1},{4,6},{6,4},{5,7},{7,5},{8,10},{10,8},{9,1... | collective-permute-start | bytes 393224 | tf_op jit(solution)/shard_map/ppermute | solution.py:497
  36.5 0.0 collective-permute-done.8.refs_1_
  36.5 1.5 %near.7.refs_7_ = f32[4,2,128,128]{3,2,1,0:T(8,128)S(1)} custom-call(f32[4,22,128,128]{3,2,1,0:T(8,128)S(1)} %phases.7.phase_ref.refs_3_, f32[32,1024]{1,0:T(8,128)S(1)} %join.11.refs_0_, f32[32,1024]{1,0:T(8,128)S(1)} %collective-permute-done.8.refs_1_), custom_call_target="tpu_custom_call" | custom-call | tf_op jit(solution)/shard_map/near/pallas_call | solution.py:583
  38.1 0.8 %collective-permute-done.9.refs_10_ = f32[32,1024]{1,0:T(8,128)S(1)} collective-permute-done((f32[32,1024]{1,0:T(8,128)S(1)}, f32[32,1024]{1,0:T(8,128)S(1)}, u32[]{:S(2)}, u32[]{:S(2)}) %collective-permute-start.9) | collective-permute-done | bytes 131104 | tf_op jit(solution)/shard_map/ppermute | solution.py:497
  38.9 0.0 collective-permute-start.11
  38.9 0.0 collective-permute-done.4.refs_1_
  38.9 0.8 %near.5.refs_5_ = f32[2,2,128,128]{3,2,1,0:T(8,128)S(1)} custom-call(f32[2,22,128,128]{3,2,1,0:T(8,128)S(1)} %phases.5.phase_ref.refs_1_, f32[32,1024]{1,0:T(8,128)S(1)} %join.8.refs_0_, f32[32,1024]{1,0:T(8,128)S(1)} %collective-permute-done.4.refs_1_), custom_call_target="tpu_custom_call" | custom-call | tf_op jit(solution)/shard_map/near/pallas_call | solution.py:583
  39.7 2.3 %near.4.refs_4_ = f32[6,2,128,128]{3,2,1,0:T(8,128)S(1)} custom-call(f32[6,22,128,128]{3,2,1,0:T(8,128)S(1)} %phases.4.phase_ref.refs_0_, f32[32,1024]{1,0:T(8,128)S(1)} %join.8.refs_0_, f32[32,1024]{1,0:T(8,128)S(1)} %collective-permute-done.4.refs_1_), custom_call_target="tpu_custom_call" | custom-call | tf_op jit(solution)/shard_map/near/pallas_call | solution.py:583
  42.0 1.6 %near.6.refs_6_ = f32[4,2,128,128]{3,2,1,0:T(8,128)S(1)} custom-call(f32[4,22,128,128]{3,2,1,0:T(8,128)S(1)} %phases.6.phase_ref.refs_2_, f32[32,1024]{1,0:T(8,128)S(1)} %join.11.refs_0_, f32[32,1024]{1,0:T(8,128)S(1)} %collective-permute-done.8.refs_1_), custom_call_target="tpu_custom_call" | custom-call | tf_op jit(solution)/shard_map/near/pallas_call | solution.py:583
  43.6 0.0 collective-permute-done.3.refs_8_
  43.6 0.6 %collective-permute-start.10 = (f32[32,1024]{1,0:T(8,128)S(1)}, f32[32,1024]{1,0:T(8,128)S(1)}, u32[]{:S(2)}, u32[]{:S(2)}) collective-permute-start(f32[32,1024]{1,0:T(8,128)S(1)} %collective-permute-done.3.refs_8_), channel_id=1, source_target_pairs={{0,1},{1,0},{2,3},{3,2},{4,5},{5,4},{6,7},{7,6},{8,9},{9,8},{10,11... | collective-permute-start | bytes 393224 | tf_op jit(solution)/shard_map/ppermute | solution.py:497
  44.2 0.0 collective-permute-done.11.refs_11_
  44.2 1.0 %collective-permute-done.10.refs_9_ = f32[32,1024]{1,0:T(8,128)S(1)} collective-permute-done((f32[32,1024]{1,0:T(8,128)S(1)}, f32[32,1024]{1,0:T(8,128)S(1)}, u32[]{:S(2)}, u32[]{:S(2)}) %collective-permute-start.10) | collective-permute-done | bytes 131104 | tf_op jit(solution)/shard_map/ppermute | solution.py:497
  45.2 7.1 %far.1 = f32[4096,128]{1,0:T(8,128)} custom-call(f32[6,22,128,128]{3,2,1,0:T(8,128)S(1)} %phases.4.phase_ref.refs_0_, f32[2,22,128,128]{3,2,1,0:T(8,128)S(1)} %phases.5.phase_ref.refs_1_, f32[4,22,128,128]{3,2,1,0:T(8,128)S(1)} %phases.6.phase_ref.refs_2_, f32[4,22,128,128]{3,2,1,0:T(8,128)S(1)} %phases.7.phase_ref.refs_3_, ...), custom_call_target="tpu_custom_call" | custom-call | tf_op jit(solution)/shard_map/far/pallas_call | solution.py:626
Async XLA Ops:
  8.1 7.4 %collective-permute-start.5 = (f32[32,1024]{1,0:T(8,128)S(1)}, f32[32,1024]{1,0:T(8,128)S(1)}, u32[]{:S(2)}, u32[]{:S(2)}) collective-permute-start(f32[32,1024]{1,0:T(8,128)S(1)} %get-tuple-element.48.own_ref), channel_id=1, source_target_pairs={{0,4},{4,0},{8,12},{12,8},{16,20},{20,16},{24,28},{28,24},{1,5},{5... | collective-permute-start | bytes 393224 | tf_op jit(solution)/shard_map/ppermute | solution.py:497
  11.1 6.7 %collective-permute-start = (f32[32,1024]{1,0:T(8,128)S(1)}, f32[32,1024]{1,0:T(8,128)S(1)}, u32[]{:S(2)}, u32[]{:S(2)}) collective-permute-start(f32[32,1024]{1,0:T(8,128)S(1)} %get-tuple-element.35.after_ref.own_ref), channel_id=1, source_target_pairs={{0,4},{4,0},{8,12},{12,8},{16,20},{20,16},{24,28},{28,24},{1,5},{5... | collective-permute-start | bytes 393224 | tf_op jit(solution)/shard_map/ppermute | solution.py:497
  15.7 6.3 %collective-permute-start.6 = (f32[32,1024]{1,0:T(8,128)S(1)}, f32[32,1024]{1,0:T(8,128)S(1)}, u32[]{:S(2)}, u32[]{:S(2)}) collective-permute-start(f32[32,1024]{1,0:T(8,128)S(1)} %join.9.own_ref), channel_id=1, source_target_pairs={{0,8},{8,0},{4,12},{12,4},{16,24},{24,16},{20,28},{28,20},{1,9},{9... | collective-permute-start | bytes 393224 | tf_op jit(solution)/shard_map/ppermute | solution.py:497
  18.0 7.4 %collective-permute-start.1 = (f32[32,1024]{1,0:T(8,128)S(1)}, f32[32,1024]{1,0:T(8,128)S(1)}, u32[]{:S(2)}, u32[]{:S(2)}) collective-permute-start(f32[32,1024]{1,0:T(8,128)S(1)} %join.6.after_ref.own_ref), channel_id=1, source_target_pairs={{0,8},{8,0},{4,12},{12,4},{16,24},{24,16},{20,28},{28,20},{1,9},{9... | collective-permute-start | bytes 393224 | tf_op jit(solution)/shard_map/ppermute | solution.py:497
  22.1 11.4 %collective-permute-start.7 = (f32[32,1024]{1,0:T(8,128)S(1)}, f32[32,1024]{1,0:T(8,128)S(1)}, u32[]{:S(2)}, u32[]{:S(2)}) collective-permute-start(f32[32,1024]{1,0:T(8,128)S(1)} %join.10.own_ref), channel_id=1, source_target_pairs={{0,16},{16,0},{4,20},{20,4},{8,24},{24,8},{12,28},{28,12},{1,17},{... | collective-permute-start | bytes 393224 | tf_op jit(solution)/shard_map/ppermute | solution.py:497
  25.6 9.5 %collective-permute-start.2 = (f32[32,1024]{1,0:T(8,128)S(1)}, f32[32,1024]{1,0:T(8,128)S(1)}, u32[]{:S(2)}, u32[]{:S(2)}) collective-permute-start(f32[32,1024]{1,0:T(8,128)S(1)} %join.7.after_ref.own_ref), channel_id=1, source_target_pairs={{0,16},{16,0},{4,20},{20,4},{8,24},{24,8},{12,28},{28,12},{1,17},{... | collective-permute-start | bytes 393224 | tf_op jit(solution)/shard_map/ppermute | solution.py:497
  33.7 5.3 %collective-permute-start.9 = (f32[32,1024]{1,0:T(8,128)S(1)}, f32[32,1024]{1,0:T(8,128)S(1)}, u32[]{:S(2)}, u32[]{:S(2)}) collective-permute-start(f32[32,1024]{1,0:T(8,128)S(1)} %join.11.refs_0_), channel_id=1, source_target_pairs={{0,2},{2,0},{1,3},{3,1},{4,6},{6,4},{5,7},{7,5},{8,10},{10,8},{9,1... | collective-permute-start | bytes 393224 | tf_op jit(solution)/shard_map/ppermute | solution.py:497
  35.0 1.5 %collective-permute-start.8 = (f32[32,1024]{1,0:T(8,128)S(1)}, f32[32,1024]{1,0:T(8,128)S(1)}, u32[]{:S(2)}, u32[]{:S(2)}) collective-permute-start(f32[32,1024]{1,0:T(8,128)S(1)} %join.11.refs_0_), channel_id=1, source_target_pairs={{0,1},{1,0},{2,3},{3,2},{4,5},{5,4},{6,7},{7,6},{8,9},{9,8},{10,11... | collective-permute-start | bytes 393224 | tf_op jit(solution)/shard_map/ppermute | solution.py:497
  35.2 3.7 %collective-permute-start.4 = (f32[32,1024]{1,0:T(8,128)S(1)}, f32[32,1024]{1,0:T(8,128)S(1)}, u32[]{:S(2)}, u32[]{:S(2)}) collective-permute-start(f32[32,1024]{1,0:T(8,128)S(1)} %join.8.refs_0_), channel_id=1, source_target_pairs={{0,1},{1,0},{2,3},{3,2},{4,5},{5,4},{6,7},{7,6},{8,9},{9,8},{10,11... | collective-permute-start | bytes 393224 | tf_op jit(solution)/shard_map/ppermute | solution.py:497
  35.8 7.8 %collective-permute-start.3 = (f32[32,1024]{1,0:T(8,128)S(1)}, f32[32,1024]{1,0:T(8,128)S(1)}, u32[]{:S(2)}, u32[]{:S(2)}) collective-permute-start(f32[32,1024]{1,0:T(8,128)S(1)} %join.8.refs_0_), channel_id=1, source_target_pairs={{0,2},{2,0},{1,3},{3,1},{4,6},{6,4},{5,7},{7,5},{8,10},{10,8},{9,1... | collective-permute-start | bytes 393224 | tf_op jit(solution)/shard_map/ppermute | solution.py:497
  38.9 5.3 %collective-permute-start.11 = (f32[32,1024]{1,0:T(8,128)S(1)}, f32[32,1024]{1,0:T(8,128)S(1)}, u32[]{:S(2)}, u32[]{:S(2)}) collective-permute-start(f32[32,1024]{1,0:T(8,128)S(1)} %collective-permute-done.9.refs_10_), channel_id=1, source_target_pairs={{0,1},{1,0},{2,3},{3,2},{4,5},{5,4},{6,7},{7,6},{8,9},{9,8},{10,11... | collective-permute-start | bytes 393224 | tf_op jit(solution)/shard_map/ppermute | solution.py:497
  43.6 1.5 %collective-permute-start.10 = (f32[32,1024]{1,0:T(8,128)S(1)}, f32[32,1024]{1,0:T(8,128)S(1)}, u32[]{:S(2)}, u32[]{:S(2)}) collective-permute-start(f32[32,1024]{1,0:T(8,128)S(1)} %collective-permute-done.3.refs_8_), channel_id=1, source_target_pairs={{0,1},{1,0},{2,3},{3,2},{4,5},{5,4},{6,7},{7,6},{8,9},{9,8},{10,11... | collective-permute-start | bytes 393224 | tf_op jit(solution)/shard_map/ppermute | solution.py:497
where the time goes:
time: 52.4 us; the launch traced here: 52.2 us
  Pallas kernels  32.3 us (62%)
  starting transfers between devices  15.9 us (30%)
  waiting for transfers between devices  3.93 us (8%)
    ppermute x12, starting transfers between devices, partner_2(): return lax.ppermute(block, axis, route)  15.9 us
    pallas_call x4, Pallas kernels, make_phases(): pl.pallas_call(functools.partial(phase_kernel, first_tile=firsts[number],...  9.95 us
    pallas_call x1, Pallas kernels, local(): pl.pallas_call(functools.partial(far_kernel, masks=masks), out_shape=jax....  7.07 us
    pallas_call x4, Pallas kernels, near_field(): pl.pallas_call(functools.partial(near_kernel, first_column=places[number]...  6.2 us
    pallas_call x1, Pallas kernels, local(): pl.pallas_call(leaf_kernel, grid=(LEAF_STEPS,), out_shape=[pltpu.VMEM((ti...  5.76 us
    ppermute x12, waiting for transfers between devices, partner_2(): return lax.ppermute(block, axis, route)  3.93 us
    pallas_call x1, Pallas kernels, local(): pl.pallas_call(tree_kernel, out_shape=[pltpu.VMEM((ROWS, box_count // CHU...  2.31 us
    pallas_call x6, Pallas kernels, join(): pl.pallas_call(functools.partial(join_kernel, bit_no=bit_no), out_shape=p...  1.05 us
  transfers between devices with their start and end apart: 12, of which 5 were waited for; matrix products, arithmetic and copies ran while one was open for 0% of the time, Pallas kernels for 33%

commit v1 on v0

--- a/solution.py
+++ b/solution.py
@@ -18,9 +18,11 @@
 ROWS = 2 * R
 HALF = R // 2
 CHUNKS = 2
-PHASE_SHARES = ((6, 0), (2, 0), (4, 1), (4, 1))
-PHASE_PLAN = {"bit_0": (0,), "bit_1": (1,), "last": (2, 3)}
+PHASE_SHARES = ((6, 0), (2, 0), (4, 1), (2, 1), (2, 1))
+PHASE_PLAN = {"bit_0": (0,), "bit_1": (1,), "last": (2, 3, 4)}
 LEAF_STEPS = 4
+LEAF_AHEAD = 2
+ROW_CHUNK = 64
 
 SIN_COEFS = (4.44288292, -7.30824569, 3.60635422, -0.84611165, 0.10982452)
 COS_COEFS = (1.4142135, -6.97885095, 5.73946038, -1.88355791, 0.31068803)
@@ -162,16 +164,20 @@
 
 
 def swap_bits(blocks, block_bit, lane_bit):
-    step = 1 << lane_bit
-    shape = blocks[0].shape
-    upper = (lax.broadcasted_iota(jnp.int32, shape, 1) >> lane_bit & 1) == 1
+    lane = lax.broadcasted_iota(jnp.int32, (8, LANES), 1)
+    upper = (lax.broadcasted_iota(jnp.int32, blocks[0].shape, 1) >> lane_bit & 1) == 1
     swapped = list(blocks)
     for number in range(len(blocks)):
         if not number >> block_bit & 1:
             other = number | 1 << block_bit
             low, high = blocks[number], blocks[other]
-            swapped[number] = jnp.where(upper, pltpu.roll(high, step, 1), low)
-            swapped[other] = jnp.where(upper, high, pltpu.roll(low, LANES - step, 1))
+            mixed = jnp.where(upper, low, high)
+            moved = jnp.concatenate(
+                [pick_lanes(mixed[row : row + 8], lane ^ 1 << lane_bit) for row in range(0, ROWS, 8)],
+                axis=0,
+            )
+            swapped[number] = jnp.where(upper, moved, low)
+            swapped[other] = jnp.where(upper, high, moved)
     return swapped
 
 
@@ -221,23 +227,45 @@
     )
 
 
-def leaf_kernel(pos_ref, strength_ref, table_ref, *refs):
-    count = (len(refs) - 2) // 2
-    out_ref, semaphores = refs[count], refs[-1]
-    copies = [
-        pltpu.make_async_copy(source, target, semaphores.at[number])
-        for number, (source, target) in enumerate(zip(refs[:count], refs[count + 1 : -1]))
+def sublane_sums(values):
+    sublane = lax.broadcasted_iota(jnp.int32, (8, LANES), 0)
+    for step in (4, 2, 1):
+        lower = (sublane & step) == 0
+        values = [
+            jnp.where(lower, first, second)
+            + pltpu.roll(jnp.where(lower, second, first), step, 0)
+            if step == 4
+            else jnp.where(lower, first, second)
+            + jnp.where(lower, pltpu.roll(first, 8 - step, 0), pltpu.roll(second, step, 0))
+            for first, second in zip(values[:step], values[step:])
+        ]
+    return values[0]
+
+
+def leaf_kernel(pos_hbm, strength_hbm, table_hbm, *refs):
+    count = (len(refs) - 8) // 2
+    out_ref, pos_ref, strength_ref, table_ref = refs[count], *refs[2 * count + 1 : 2 * count + 4]
+    pos_done, strength_done, table_done, other_done = refs[2 * count + 4 :]
+    others = [
+        pltpu.make_async_copy(source, target, other_done.at[number])
+        for number, (source, target) in enumerate(zip(refs[:count], refs[count + 1 :]))
     ]
-
-    @pl.when(pl.program_id(0) == 0)
-    def start_copies():
-        for copy in copies:
+    table_copy = pltpu.make_async_copy(table_hbm, table_ref, table_done)
+    size = pos_ref.shape[0] // LEAF_STEPS
+
+    def step_copies(step):
+        rows = pl.ds(pl.multiple_of(step * size, LANES), size)
+        yield pltpu.make_async_copy(pos_hbm.at[rows, :], pos_ref.at[rows, :], pos_done.at[step])
+        yield pltpu.make_async_copy(
+            strength_hbm.at[:, rows, :], strength_ref.at[:, rows, :], strength_done.at[step]
+        )
+
+    table_copy.start()
+    for step in range(LEAF_AHEAD):
+        for copy in step_copies(step):
             copy.start()
 
-    tile_count = pos_ref.shape[0] // LANES
-    first = pl.program_id(0) * tile_count
-
-    def one_tile(tile, carry):
+    def one_tile(tile):
         parts = [[], [], []]
         for group in range(16):
             start = tile * LANES + 8 * reverse_bits(group, 4)
@@ -264,16 +292,31 @@
                         term = base if inner is None else base * inner
                         row = side * R + 4 * high + low
                         sums[row] = term if sums[row] is None else sums[row] + term
-        for row in range(ROWS):
-            out_ref[first + tile, pl.ds(row, 1), :] = jnp.sum(sums[row], axis=0, keepdims=True)
+        for row in range(0, ROWS, 8):
+            out_ref[tile, pl.ds(row, 8), :] = sublane_sums(sums[row : row + 8])
+
+    def one_step(step, carry):
+        for copy in step_copies(step):
+            copy.wait()
+
+        @pl.when(step < LEAF_STEPS - LEAF_AHEAD)
+        def start_later():
+            for copy in step_copies(step + LEAF_AHEAD):
+                copy.start()
+
+        @pl.when(step == LEAF_STEPS - LEAF_AHEAD)
+        def start_others():
+            for copy in others:
+                copy.start()
+
+        for tile in range(size // LANES):
+            one_tile(step * (size // LANES) + tile)
         return carry
 
-    lax.fori_loop(0, tile_count, one_tile, 0, unroll=4)
-
-    @pl.when(pl.program_id(0) == pl.num_programs(0) - 1)
-    def wait_copies():
-        for copy in copies:
-            copy.wait()
+    table_copy.wait()
+    lax.fori_loop(0, LEAF_STEPS, one_step, 0)
+    for copy in others:
+        copy.wait()
 
 
 def tree_kernel(moment_ref, t1_ref, t2_ref, t3_ref, t4_ref, *out_refs):
@@ -374,11 +417,11 @@
     lax.fori_loop(0, out_ref.shape[0], one_tile, 0, unroll=2)
 
 
-def block_sums(phase_ref, roots, tile, first):
+def block_sums(phase_ref, roots, tile, rows, first):
     totals = [None, None]
     for node in range(HALF):
         for wave in range(2):
-            phase = phase_ref[tile, 2 * node + wave]
+            phase = phase_ref[tile, 2 * node + wave, rows, :]
             for side in range(2):
                 row = first + (2 * side + wave) * HALF + node
                 term = phase * roots[pl.ds(row, 1), :]
@@ -391,16 +434,17 @@
     for number, root_ref in enumerate(root_refs):
         rows = pl.ds((low ^ number) * ROWS, ROWS)
         roots[rows, :] = root_ref[:, pl.ds(pl.multiple_of(column, LANES), LANES)]
-    for side, total in enumerate(block_sums(phase_ref, roots, tile, ROWS)):
-        sums[side] = total
-    totals = block_sums(phase_ref, roots, tile, 0)
-    step = phase_ref[tile, 2 * HALF], phase_ref[tile, 2 * HALF + 1]
-    real, imag = complex_product(step, (sums[0], sums[1]))
     plane = 2 * HALF + 2 + 2 * pair
-    start = phase_ref[tile, plane], phase_ref[tile, plane + 1]
-    values = complex_product(start, (real + totals[0], imag + totals[1]))
-    for side, value in enumerate(values):
-        sums[side] = value if add_ref is None else value + add_ref[side]
+    for first in range(0, TGT_BOX, ROW_CHUNK):
+        rows = slice(first, first + ROW_CHUNK)
+        high = block_sums(phase_ref, roots, tile, rows, ROWS)
+        step = phase_ref[tile, 2 * HALF, rows, :], phase_ref[tile, 2 * HALF + 1, rows, :]
+        real, imag = complex_product(step, high)
+        low_real, low_imag = block_sums(phase_ref, roots, tile, rows, 0)
+        start = phase_ref[tile, plane, rows, :], phase_ref[tile, plane + 1, rows, :]
+        values = complex_product(start, (real + low_real, imag + low_imag))
+        for side, value in enumerate(values):
+            sums[side, rows, :] = value if add_ref is None else value + add_ref[side, rows, :]
 
 
 def near_kernel(phase_ref, *refs, first_column):
@@ -513,24 +557,25 @@
     part_tiles = [tile_count * share // 16 for share, _ in PHASE_SHARES]
     firsts, places = share_places(part_tiles)
 
-    leaf_rows = box_count // LEAF_STEPS
     tables = source_tables() + [
         join_table(local_depth + bit_no, bit_no == leaf_bits - 1) for bit_no in range(leaf_bits)
     ]
     copied = [*tables, tgt_pos.reshape(box_count, TGT_BOX)]
     moments, *copied = pl.pallas_call(
         leaf_kernel,
-        grid=(LEAF_STEPS,),
         out_shape=[pltpu.VMEM((tile_count, ROWS, LANES), jnp.float32)]
         + [pltpu.VMEM(value.shape, value.dtype) for value in copied],
-        in_specs=[
-            pl.BlockSpec((leaf_rows, PER_BOX), lambda i: (i, 0)),
-            pl.BlockSpec((2, leaf_rows, PER_BOX), lambda i: (0, i, 0)),
-            pl.BlockSpec((16, BOX_CELLS), lambda i: (0, 0)),
-        ]
-        + [pl.BlockSpec(memory_space=pl.ANY)] * len(copied),
+        in_specs=[pl.BlockSpec(memory_space=pl.ANY)] * (3 + len(copied)),
         out_specs=whole_vmem(1 + len(copied)),
-        scratch_shapes=[pltpu.SemaphoreType.DMA((len(copied),))],
+        scratch_shapes=[
+            pltpu.VMEM((box_count, PER_BOX), jnp.int32),
+            pltpu.VMEM((2, box_count, PER_BOX), jnp.float32),
+            pltpu.VMEM((16, BOX_CELLS), jnp.float32),
+            pltpu.SemaphoreType.DMA((LEAF_STEPS,)),
+            pltpu.SemaphoreType.DMA((LEAF_STEPS,)),
+            pltpu.SemaphoreType.DMA,
+            pltpu.SemaphoreType.DMA((len(copied),)),
+        ],
         compiler_params=small_vmem,
         name="leaves",
     )(

time: 52.4 us -> 51.1 us (0.975)
  Pallas kernels: 32.3 us -> 30.6 us
    pallas_call x4 -> x5, Pallas kernels: 6.2 us -> 4.91 us  [near_field(): pl.pallas_call(functools.partial(near_kernel, first_column=places[number]...]
    pallas_call x4 -> x5, Pallas kernels: 9.95 us -> 9.82 us  [make_phases(): pl.pallas_call(functools.partial(phase_kernel, first_tile=firsts[number],...]
  transfers between devices with their start and end apart: 12 -> 12, of which waited for: 5 -> 5; matrix products, arithmetic and copies ran while one was open for 0% -> 0% of each run, Pallas kernels for 33% -> 31%
where the time goes in v1:
time: 51.1 us; the launch traced here: 50.9 us
  Pallas kernels  30.6 us (60%)
  starting transfers between devices  15.9 us (31%)
  waiting for transfers between devices  4.41 us (9%)
    ppermute x12, starting transfers between devices, partner_2(): return lax.ppermute(block, axis, route)  15.9 us
    pallas_call x5, Pallas kernels, make_phases(): pl.pallas_call(functools.partial(phase_kernel, first_tile=firsts[number],...  9.82 us
    pallas_call x1, Pallas kernels, local(): pl.pallas_call(functools.partial(far_kernel, masks=masks), out_shape=jax....  7.02 us
    pallas_call x1, Pallas kernels, local(): pl.pallas_call(leaf_kernel, out_shape=[pltpu.VMEM((tile_count, ROWS, LANE...  5.42 us
    pallas_call x5, Pallas kernels, near_field(): pl.pallas_call(functools.partial(near_kernel, first_column=places[number]...  4.91 us
    ppermute x12, waiting for transfers between devices, partner_2(): return lax.ppermute(block, axis, route)  4.41 us
    pallas_call x1, Pallas kernels, local(): pl.pallas_call(tree_kernel, out_shape=[pltpu.VMEM((ROWS, box_count // CHU...  2.34 us
    pallas_call x6, Pallas kernels, join(): pl.pallas_call(functools.partial(join_kernel, bit_no=bit_no), out_shape=p...  1.05 us
  transfers between devices with their start and end apart: 12, of which 5 were waited for; matrix products, arithmetic and copies ran while one was open for 0% of the time, Pallas kernels for 31%

profile of v1, /device:TPU:0, one launch (start us, length us, event | category | flops | bytes accessed | tf_op | source)
XLA Modules:
  0.0 50.9 jit_solution(7888362053800498123)
XLA Ops:
  0.0 5.4 %leaves.1 = (f32[16,32,128]{2,1,0:T(8,128)S(1)}, bf16[256,768]{1,0:T(8,128)(2,1)S(1)}, bf16[256,768]{1,0:T(8,128)(2,1)S(1)}, bf16[256,768]{1,0:T(8,128)(2,1)S(1)...) custom-call(s32[2048,128]{1,0:T(8,128)} %bitcast.9, ...), custom_call_target="tpu_custom_call" | custom-call | tf_op jit(solution)/shard_map/leaves/pallas_call | solution.py:564
  5.4 2.3 %tree.1 = (f32[32,1024]{1,0:T(8,128)S(1)}, f32[32,1024]{1,0:T(8,128)S(1)}) custom-call(f32[16,32,128]{2,1,0:T(8,128)S(1)} %get-tuple-element.32.moment_ref, bf16[256,768]{1,0:T(8,128)(2,1)S(1)} %get-tuple-element.33.t1_ref, bf16[256,768]{1,0:T(8,128)(2,1)S(1)} %get-tuple-element.34.t2_ref, bf16[256,768]{1,0:T(8,128)(2,1)S(1)} %get-tuple-element.35.t3_ref, ...), custom_call_target="tpu_custom_call" | custom-call | tf_op jit(solution)/shard_map/tree/pallas_call | solution.py:588
  7.8 3.1 %collective-permute-start.5 = (f32[32,1024]{1,0:T(8,128)S(1)}, f32[32,1024]{1,0:T(8,128)S(1)}, u32[]{:S(2)}, u32[]{:S(2)}) collective-permute-start(f32[32,1024]{1,0:T(8,128)S(1)} %get-tuple-element.52.own_ref), channel_id=1, source_target_pairs={{0,4},{4,0},{8,12},{12,8},{16,20},{20,16},{24,28},{28,24},{1,5},{5... | collective-permute-start | bytes 393224 | tf_op jit(solution)/shard_map/ppermute | solution.py:541
  10.8 0.1 collective-permute-start
  10.9 3.7 %phases.5.phase_ref.refs_0_ = f32[6,22,128,128]{3,2,1,0:T(8,128)S(1)} custom-call(s32[2048,128]{1,0:T(8,128)S(1)} %get-tuple-element.38.tgt_ref, f32[32,1024]{1,0:T(8,128)S(1)} %get-tuple-element.37.after_ref.own_ref), custom_call_target="tpu_custom_call" | custom-call | tf_op jit(solution)/shard_map/phases/pallas_call | solution.py:602
  14.7 0.5 %collective-permute-done.5.partner_ref = f32[32,1024]{1,0:T(8,128)S(1)} collective-permute-done((f32[32,1024]{1,0:T(8,128)S(1)}, f32[32,1024]{1,0:T(8,128)S(1)}, u32[]{:S(2)}, u32[]{:S(2)}) %collective-permute-start.5) | collective-permute-done | bytes 131104 | tf_op jit(solution)/shard_map/ppermute | solution.py:541
  15.2 0.2 join.9.own_ref
  15.4 2.1 %collective-permute-start.6 = (f32[32,1024]{1,0:T(8,128)S(1)}, f32[32,1024]{1,0:T(8,128)S(1)}, u32[]{:S(2)}, u32[]{:S(2)}) collective-permute-start(f32[32,1024]{1,0:T(8,128)S(1)} %join.9.own_ref), channel_id=1, source_target_pairs={{0,8},{8,0},{4,12},{12,4},{16,24},{24,16},{20,28},{28,20},{1,9},{9... | collective-permute-start | bytes 393224 | tf_op jit(solution)/shard_map/ppermute | solution.py:541
  17.5 0.0 collective-permute-done.partner_ref
  17.5 0.2 join.6.after_ref.own_ref
  17.7 1.5 %collective-permute-start.1 = (f32[32,1024]{1,0:T(8,128)S(1)}, f32[32,1024]{1,0:T(8,128)S(1)}, u32[]{:S(2)}, u32[]{:S(2)}) collective-permute-start(f32[32,1024]{1,0:T(8,128)S(1)} %join.6.after_ref.own_ref), channel_id=1, source_target_pairs={{0,8},{8,0},{4,12},{12,4},{16,24},{24,16},{20,28},{28,20},{1,9},{9... | collective-permute-start | bytes 393224 | tf_op jit(solution)/shard_map/ppermute | solution.py:541
  19.2 1.2 %phases.6.phase_ref.refs_1_ = f32[2,22,128,128]{3,2,1,0:T(8,128)S(1)} custom-call(s32[2048,128]{1,0:T(8,128)S(1)} %get-tuple-element.38.tgt_ref, f32[32,1024]{1,0:T(8,128)S(1)} %join.6.after_ref.own_ref), custom_call_target="tpu_custom_call" | custom-call | tf_op jit(solution)/shard_map/phases/pallas_call | solution.py:602
  20.4 1.3 %collective-permute-done.6.partner_ref = f32[32,1024]{1,0:T(8,128)S(1)} collective-permute-done((f32[32,1024]{1,0:T(8,128)S(1)}, f32[32,1024]{1,0:T(8,128)S(1)}, u32[]{:S(2)}, u32[]{:S(2)}) %collective-permute-start.6) | collective-permute-done | bytes 131104 | tf_op jit(solution)/shard_map/ppermute | solution.py:541
  21.7 0.2 join.10.own_ref
  21.8 3.3 %collective-permute-start.7 = (f32[32,1024]{1,0:T(8,128)S(1)}, f32[32,1024]{1,0:T(8,128)S(1)}, u32[]{:S(2)}, u32[]{:S(2)}) collective-permute-start(f32[32,1024]{1,0:T(8,128)S(1)} %join.10.own_ref), channel_id=1, source_target_pairs={{0,16},{16,0},{4,20},{20,4},{8,24},{24,8},{12,28},{28,12},{1,17},{... | collective-permute-start | bytes 393224 | tf_op jit(solution)/shard_map/ppermute | solution.py:541
  25.1 0.0 collective-permute-done.1.partner_ref
  25.1 0.2 join.7.after_ref.own_ref
  25.3 2.6 %collective-permute-start.2 = (f32[32,1024]{1,0:T(8,128)S(1)}, f32[32,1024]{1,0:T(8,128)S(1)}, u32[]{:S(2)}, u32[]{:S(2)}) collective-permute-start(f32[32,1024]{1,0:T(8,128)S(1)} %join.7.after_ref.own_ref), channel_id=1, source_target_pairs={{0,16},{16,0},{4,20},{20,4},{8,24},{24,8},{12,28},{28,12},{1,17},{... | collective-permute-start | bytes 393224 | tf_op jit(solution)/shard_map/ppermute | solution.py:541
  27.9 1.2 %phases.9.phase_ref.refs_4_ = f32[2,22,128,128]{3,2,1,0:T(8,128)S(1)} custom-call(s32[2048,128]{1,0:T(8,128)S(1)} %get-tuple-element.38.tgt_ref, f32[32,1024]{1,0:T(8,128)S(1)} %join.7.after_ref.own_ref), custom_call_target="tpu_custom_call" | custom-call | tf_op jit(solution)/shard_map/phases/pallas_call | solution.py:602
  29.1 1.2 %phases.8.phase_ref.refs_3_ = f32[2,22,128,128]{3,2,1,0:T(8,128)S(1)} custom-call(s32[2048,128]{1,0:T(8,128)S(1)} %get-tuple-element.38.tgt_ref, f32[32,1024]{1,0:T(8,128)S(1)} %join.7.after_ref.own_ref), custom_call_target="tpu_custom_call" | custom-call | tf_op jit(solution)/shard_map/phases/pallas_call | solution.py:602
  30.3 2.5 %phases.7.phase_ref.refs_2_ = f32[4,22,128,128]{3,2,1,0:T(8,128)S(1)} custom-call(s32[2048,128]{1,0:T(8,128)S(1)} %get-tuple-element.38.tgt_ref, f32[32,1024]{1,0:T(8,128)S(1)} %join.7.after_ref.own_ref), custom_call_target="tpu_custom_call" | custom-call | tf_op jit(solution)/shard_map/phases/pallas_call | solution.py:602
  32.8 0.4 collective-permute-done.7.partner_ref
  33.2 0.2 join.11.refs_0_
  33.4 1.4 %collective-permute-start.9 = (f32[32,1024]{1,0:T(8,128)S(1)}, f32[32,1024]{1,0:T(8,128)S(1)}, u32[]{:S(2)}, u32[]{:S(2)}) collective-permute-start(f32[32,1024]{1,0:T(8,128)S(1)} %join.11.refs_0_), channel_id=1, source_target_pairs={{0,2},{2,0},{1,3},{3,1},{4,6},{6,4},{5,7},{7,5},{8,10},{10,8},{9,1... | collective-permute-start | bytes 393224 | tf_op jit(solution)/shard_map/ppermute | solution.py:541
  34.7 0.0 collective-permute-start.8
  34.7 0.0 collective-permute-done.2.partner_ref
  34.7 0.2 join.8.refs_0_
  34.9 0.6 %collective-permute-start.4 = (f32[32,1024]{1,0:T(8,128)S(1)}, f32[32,1024]{1,0:T(8,128)S(1)}, u32[]{:S(2)}, u32[]{:S(2)}) collective-permute-start(f32[32,1024]{1,0:T(8,128)S(1)} %join.8.refs_0_), channel_id=1, source_target_pairs={{0,1},{1,0},{2,3},{3,2},{4,5},{5,4},{6,7},{7,6},{8,9},{9,8},{10,11... | collective-permute-start | bytes 393224 | tf_op jit(solution)/shard_map/ppermute | solution.py:541
  35.5 0.7 %collective-permute-start.3 = (f32[32,1024]{1,0:T(8,128)S(1)}, f32[32,1024]{1,0:T(8,128)S(1)}, u32[]{:S(2)}, u32[]{:S(2)}) collective-permute-start(f32[32,1024]{1,0:T(8,128)S(1)} %join.8.refs_0_), channel_id=1, source_target_pairs={{0,2},{2,0},{1,3},{3,1},{4,6},{6,4},{5,7},{7,5},{8,10},{10,8},{9,1... | collective-permute-start | bytes 393224 | tf_op jit(solution)/shard_map/ppermute | solution.py:541
  36.2 0.0 collective-permute-done.8.refs_1_
  36.2 0.6 %near.8.refs_8_ = f32[2,2,128,128]{3,2,1,0:T(8,128)S(1)} custom-call(f32[2,22,128,128]{3,2,1,0:T(8,128)S(1)} %phases.8.phase_ref.refs_3_, f32[32,1024]{1,0:T(8,128)S(1)} %join.11.refs_0_, f32[32,1024]{1,0:T(8,128)S(1)} %collective-permute-done.8.refs_1_), custom_call_target="tpu_custom_call" | custom-call | tf_op jit(solution)/shard_map/near/pallas_call | solution.py:628
  36.8 1.8 %collective-permute-done.9.refs_12_ = f32[32,1024]{1,0:T(8,128)S(1)} collective-permute-done((f32[32,1024]{1,0:T(8,128)S(1)}, f32[32,1024]{1,0:T(8,128)S(1)}, u32[]{:S(2)}, u32[]{:S(2)}) %collective-permute-start.9) | collective-permute-done | bytes 131104 | tf_op jit(solution)/shard_map/ppermute | solution.py:541
  38.6 0.0 collective-permute-start.11
  38.6 1.2 %near.7.refs_7_ = f32[4,2,128,128]{3,2,1,0:T(8,128)S(1)} custom-call(f32[4,22,128,128]{3,2,1,0:T(8,128)S(1)} %phases.7.phase_ref.refs_2_, f32[32,1024]{1,0:T(8,128)S(1)} %join.11.refs_0_, f32[32,1024]{1,0:T(8,128)S(1)} %collective-permute-done.8.refs_1_), custom_call_target="tpu_custom_call" | custom-call | tf_op jit(solution)/shard_map/near/pallas_call | solution.py:628
  39.9 0.0 collective-permute-done.4.refs_1_
  39.9 0.6 %near.6.refs_6_ = f32[2,2,128,128]{3,2,1,0:T(8,128)S(1)} custom-call(f32[2,22,128,128]{3,2,1,0:T(8,128)S(1)} %phases.6.phase_ref.refs_1_, f32[32,1024]{1,0:T(8,128)S(1)} %join.8.refs_0_, f32[32,1024]{1,0:T(8,128)S(1)} %collective-permute-done.4.refs_1_), custom_call_target="tpu_custom_call" | custom-call | tf_op jit(solution)/shard_map/near/pallas_call | solution.py:628
  40.5 1.8 %near.5.refs_5_ = f32[6,2,128,128]{3,2,1,0:T(8,128)S(1)} custom-call(f32[6,22,128,128]{3,2,1,0:T(8,128)S(1)} %phases.5.phase_ref.refs_0_, f32[32,1024]{1,0:T(8,128)S(1)} %join.8.refs_0_, f32[32,1024]{1,0:T(8,128)S(1)} %collective-permute-done.4.refs_1_), custom_call_target="tpu_custom_call" | custom-call | tf_op jit(solution)/shard_map/near/pallas_call | solution.py:628
  42.4 0.0 collective-permute-done.3.refs_10_
  42.4 0.6 %collective-permute-start.10 = (f32[32,1024]{1,0:T(8,128)S(1)}, f32[32,1024]{1,0:T(8,128)S(1)}, u32[]{:S(2)}, u32[]{:S(2)}) collective-permute-start(f32[32,1024]{1,0:T(8,128)S(1)} %collective-permute-done.3.refs_10_), channel_id=1, source_target_pairs={{0,1},{1,0},{2,3},{3,2},{4,5},{5,4},{6,7},{7,6},{8,9},{9,8},{10,11... | collective-permute-start | bytes 393224 | tf_op jit(solution)/shard_map/ppermute | solution.py:541
  42.9 0.6 %near.9.refs_9_ = f32[2,2,128,128]{3,2,1,0:T(8,128)S(1)} custom-call(f32[2,22,128,128]{3,2,1,0:T(8,128)S(1)} %phases.9.phase_ref.refs_4_, f32[32,1024]{1,0:T(8,128)S(1)} %join.11.refs_0_, f32[32,1024]{1,0:T(8,128)S(1)} %collective-permute-done.8.refs_1_), custom_call_target="tpu_custom_call" | custom-call | tf_op jit(solution)/shard_map/near/pallas_call | solution.py:628
  43.5 0.0 collective-permute-done.11.refs_13_
  43.5 0.4 collective-permute-done.10.refs_11_
  43.9 7.0 %far.1 = f32[4096,128]{1,0:T(8,128)} custom-call(f32[6,22,128,128]{3,2,1,0:T(8,128)S(1)} %phases.5.phase_ref.refs_0_, f32[2,22,128,128]{3,2,1,0:T(8,128)S(1)} %phases.6.phase_ref.refs_1_, f32[4,22,128,128]{3,2,1,0:T(8,128)S(1)} %phases.7.phase_ref.refs_2_, f32[2,22,128,128]{3,2,1,0:T(8,128)S(1)} %phases.8.phase_ref.refs_3_, ...), custom_call_target="tpu_custom_call" | custom-call | tf_op jit(solution)/shard_map/far/pallas_call | solution.py:671
Async XLA Ops:
  7.8 7.4 %collective-permute-start.5 = (f32[32,1024]{1,0:T(8,128)S(1)}, f32[32,1024]{1,0:T(8,128)S(1)}, u32[]{:S(2)}, u32[]{:S(2)}) collective-permute-start(f32[32,1024]{1,0:T(8,128)S(1)} %get-tuple-element.52.own_ref), channel_id=1, source_target_pairs={{0,4},{4,0},{8,12},{12,8},{16,20},{20,16},{24,28},{28,24},{1,5},{5... | collective-permute-start | bytes 393224 | tf_op jit(solution)/shard_map/ppermute | solution.py:541
  10.8 6.7 %collective-permute-start = (f32[32,1024]{1,0:T(8,128)S(1)}, f32[32,1024]{1,0:T(8,128)S(1)}, u32[]{:S(2)}, u32[]{:S(2)}) collective-permute-start(f32[32,1024]{1,0:T(8,128)S(1)} %get-tuple-element.37.after_ref.own_ref), channel_id=1, source_target_pairs={{0,4},{4,0},{8,12},{12,8},{16,20},{20,16},{24,28},{28,24},{1,5},{5... | collective-permute-start | bytes 393224 | tf_op jit(solution)/shard_map/ppermute | solution.py:541
  15.4 6.3 %collective-permute-start.6 = (f32[32,1024]{1,0:T(8,128)S(1)}, f32[32,1024]{1,0:T(8,128)S(1)}, u32[]{:S(2)}, u32[]{:S(2)}) collective-permute-start(f32[32,1024]{1,0:T(8,128)S(1)} %join.9.own_ref), channel_id=1, source_target_pairs={{0,8},{8,0},{4,12},{12,4},{16,24},{24,16},{20,28},{28,20},{1,9},{9... | collective-permute-start | bytes 393224 | tf_op jit(solution)/shard_map/ppermute | solution.py:541
  17.7 7.4 %collective-permute-start.1 = (f32[32,1024]{1,0:T(8,128)S(1)}, f32[32,1024]{1,0:T(8,128)S(1)}, u32[]{:S(2)}, u32[]{:S(2)}) collective-permute-start(f32[32,1024]{1,0:T(8,128)S(1)} %join.6.after_ref.own_ref), channel_id=1, source_target_pairs={{0,8},{8,0},{4,12},{12,4},{16,24},{24,16},{20,28},{28,20},{1,9},{9... | collective-permute-start | bytes 393224 | tf_op jit(solution)/shard_map/ppermute | solution.py:541
  21.8 11.4 %collective-permute-start.7 = (f32[32,1024]{1,0:T(8,128)S(1)}, f32[32,1024]{1,0:T(8,128)S(1)}, u32[]{:S(2)}, u32[]{:S(2)}) collective-permute-start(f32[32,1024]{1,0:T(8,128)S(1)} %join.10.own_ref), channel_id=1, source_target_pairs={{0,16},{16,0},{4,20},{20,4},{8,24},{24,8},{12,28},{28,12},{1,17},{... | collective-permute-start | bytes 393224 | tf_op jit(solution)/shard_map/ppermute | solution.py:541
  25.3 9.4 %collective-permute-start.2 = (f32[32,1024]{1,0:T(8,128)S(1)}, f32[32,1024]{1,0:T(8,128)S(1)}, u32[]{:S(2)}, u32[]{:S(2)}) collective-permute-start(f32[32,1024]{1,0:T(8,128)S(1)} %join.7.after_ref.own_ref), channel_id=1, source_target_pairs={{0,16},{16,0},{4,20},{20,4},{8,24},{24,8},{12,28},{28,12},{1,17},{... | collective-permute-start | bytes 393224 | tf_op jit(solution)/shard_map/ppermute | solution.py:541
  33.4 5.3 %collective-permute-start.9 = (f32[32,1024]{1,0:T(8,128)S(1)}, f32[32,1024]{1,0:T(8,128)S(1)}, u32[]{:S(2)}, u32[]{:S(2)}) collective-permute-start(f32[32,1024]{1,0:T(8,128)S(1)} %join.11.refs_0_), channel_id=1, source_target_pairs={{0,2},{2,0},{1,3},{3,1},{4,6},{6,4},{5,7},{7,5},{8,10},{10,8},{9,1... | collective-permute-start | bytes 393224 | tf_op jit(solution)/shard_map/ppermute | solution.py:541
  34.7 1.5 %collective-permute-start.8 = (f32[32,1024]{1,0:T(8,128)S(1)}, f32[32,1024]{1,0:T(8,128)S(1)}, u32[]{:S(2)}, u32[]{:S(2)}) collective-permute-start(f32[32,1024]{1,0:T(8,128)S(1)} %join.11.refs_0_), channel_id=1, source_target_pairs={{0,1},{1,0},{2,3},{3,2},{4,5},{5,4},{6,7},{7,6},{8,9},{9,8},{10,11... | collective-permute-start | bytes 393224 | tf_op jit(solution)/shard_map/ppermute | solution.py:541
  34.9 5.0 %collective-permute-start.4 = (f32[32,1024]{1,0:T(8,128)S(1)}, f32[32,1024]{1,0:T(8,128)S(1)}, u32[]{:S(2)}, u32[]{:S(2)}) collective-permute-start(f32[32,1024]{1,0:T(8,128)S(1)} %join.8.refs_0_), channel_id=1, source_target_pairs={{0,1},{1,0},{2,3},{3,2},{4,5},{5,4},{6,7},{7,6},{8,9},{9,8},{10,11... | collective-permute-start | bytes 393224 | tf_op jit(solution)/shard_map/ppermute | solution.py:541
  35.5 6.9 %collective-permute-start.3 = (f32[32,1024]{1,0:T(8,128)S(1)}, f32[32,1024]{1,0:T(8,128)S(1)}, u32[]{:S(2)}, u32[]{:S(2)}) collective-permute-start(f32[32,1024]{1,0:T(8,128)S(1)} %join.8.refs_0_), channel_id=1, source_target_pairs={{0,2},{2,0},{1,3},{3,1},{4,6},{6,4},{5,7},{7,5},{8,10},{10,8},{9,1... | collective-permute-start | bytes 393224 | tf_op jit(solution)/shard_map/ppermute | solution.py:541
  38.6 4.9 %collective-permute-start.11 = (f32[32,1024]{1,0:T(8,128)S(1)}, f32[32,1024]{1,0:T(8,128)S(1)}, u32[]{:S(2)}, u32[]{:S(2)}) collective-permute-start(f32[32,1024]{1,0:T(8,128)S(1)} %collective-permute-done.9.refs_12_), channel_id=1, source_target_pairs={{0,1},{1,0},{2,3},{3,2},{4,5},{5,4},{6,7},{7,6},{8,9},{9,8},{10,11... | collective-permute-start | bytes 393224 | tf_op jit(solution)/shard_map/ppermute | solution.py:541
  42.4 1.5 %collective-permute-start.10 = (f32[32,1024]{1,0:T(8,128)S(1)}, f32[32,1024]{1,0:T(8,128)S(1)}, u32[]{:S(2)}, u32[]{:S(2)}) collective-permute-start(f32[32,1024]{1,0:T(8,128)S(1)} %collective-permute-done.3.refs_10_), channel_id=1, source_target_pairs={{0,1},{1,0},{2,3},{3,2},{4,5},{5,4},{6,7},{7,6},{8,9},{9,8},{10,11... | collective-permute-start | bytes 393224 | tf_op jit(solution)/shard_map/ppermute | solution.py:541
